TPU v7x, 32 devices: a whole 2x2x4 slice. The times are simulated.
32 devices in a mesh: design: 2 (over x), blk: 16 (over z, y, core).
Axes of the slice: x: 2, y: 2, z: 4, core: 2. Of those that a mesh axis runs over, the one named last changes fastest.
Arguments:
- right_side: float32 [6, 256, 1024], P(None, ('design', 'blk')), parts along dimension 1, may hold values from -6 to 6
- adjoint_start: float32 [6, 256, 1024], P(None, ('design', 'blk')), parts along dimension 1, may hold values from -3 to 3
- diag_inverse: float32 [6, 6, 256, 1024], P(None, None, ('design', 'blk')), parts along dimension 2
- face_jacobian: bfloat16 [4, 6, 6, 256, 1024], P(None, None, None, ('design', 'blk')), parts along dimension 3, may hold values from -0.25 to 0.25
- receptor_cell: int32 [32, 16, 16], P(('design', 'blk')), parts along dimension 0, may hold values from 0 to 8191
- donor_cell: int32 [32, 16, 4, 16], P(('design', 'blk')), parts along dimension 0, may hold values from 0 to 8191
- donor_weight: float32 [32, 16, 4, 16], P(('design', 'blk')), parts along dimension 0, may hold values from 0 to 1, as said below
- live_count: int32 [32, 16], P(('design', 'blk')), parts along dimension 0, may hold values from 0 to 16, as said below
Outputs:
- adjoint: float32 [6, 256, 1024], P(None, ('design', 'blk')), parts along dimension 1
- correction_norms: float32 [4], P('design'), parts along dimension 0
There are 2 independent parts, one for each index of `design`. A program takes and returns all parts, laid end to end along the dimension named above; each array names one. Nothing has to cross between parts.
Inputs may be any that keep to these rules, and one draw needn't show every extreme that they name: live_count[s, d] counts the leading live slots of list (s, d); in every draw some partition d has 16 live slots from every source s. `donor_weight`: the four weights of each slot are positive and sum to 1.
All inputs are finite; a program needn't handle non-finite values.
Results may differ from a plain program's by a relative error of at most 0.0003.
Values sent between devices are 32-bit elements; how exact they have to be, the bound alone decides.
A program may use at most 64 MiB of HBM per device.

v0:
```python
import math
import jax
import jax.numpy as jnp
from jax import lax
from jax.sharding import PartitionSpec as P

SWEEPS = 2


def padded_2(block, sides, width):
    for axis, dim in sides:
        count = lax.axis_size(axis)
        forward = [(i, i + 1) for i in range(count - 1)]
        backward = [(target, source) for source, target in forward]
        low = lax.ppermute(
            lax.slice_in_dim(block, block.shape[dim] - width, None, axis=dim), axis, forward
        )
        high = lax.ppermute(lax.slice_in_dim(block, 0, width, axis=dim), axis, backward)
        block = jnp.concatenate([low, block, high], axis=dim)
    return block


def group_count(parts, rows_each):
    best = 1
    for count in range(1, parts + 1):
        if parts % count == 0 and count * rows_each <= 2048:
            best = count
    return best


def split_index(index, width, blocks):
    upper = index // width
    lower = index - upper * width
    block_hot = (upper[:, None] == jnp.arange(blocks, dtype=jnp.int32)[None, :]).astype(jnp.float32)
    offset_hot = (lower[:, None] == jnp.arange(width, dtype=jnp.int32)[None, :]).astype(jnp.float32)
    return (block_hot, offset_hot)


def pick_cells(field, index, rows_each):
    nvar, cells = field.shape
    parts = index.shape[0] // rows_each
    width = math.gcd(cells, 128)
    blocks = cells // width
    shaped = field.reshape(nvar, blocks, width)
    members = group_count(parts, rows_each)
    grouped = index.reshape(parts // members, members * rows_each)

    def pick_one_group(rows_index):
        block_hot, offset_hot = split_index(rows_index, width, blocks)
        picked = jnp.einsum("tb,abo->tao", block_hot, shaped, precision=lax.Precision.HIGHEST)
        return jnp.sum(picked * offset_hot[:, None, :], axis=2)

    gathered = lax.map(pick_one_group, grouped)
    return jnp.transpose(gathered, (2, 0, 1)).reshape(nvar, -1)


def spread_cells(terms, index, cells, rows_each):
    nvar = terms.shape[0]
    parts = index.shape[0] // rows_each
    width = math.gcd(cells, 128)
    blocks = cells // width
    members = group_count(parts, rows_each)
    groups = parts // members
    grouped_index = index.reshape(groups, members * rows_each)
    grouped_terms = jnp.transpose(terms.reshape(nvar, groups, members * rows_each), (1, 0, 2))

    def spread_one_group(total, pieces):
        rows_index, rows_terms = pieces
        block_hot, offset_hot = split_index(rows_index, width, blocks)
        weighted = rows_terms[:, :, None] * block_hot[None]
        added = jnp.einsum("atb,to->abo", weighted, offset_hot, precision=lax.Precision.HIGHEST)
        return (total + added, None)

    start = jnp.zeros((nvar, blocks, width), jnp.float32)
    total, unused = lax.scan(spread_one_group, start, (grouped_index, grouped_terms))
    return total.reshape(nvar, cells)


def face_coupling(psi, face_jacobian):
    padded = padded_2(psi, (("blk", 1),), 1)
    widened = jnp.pad(psi, ((0, 0), (0, 0), (1, 1)))
    sides = (padded[:, :-2, :], padded[:, 2:, :], widened[:, :, :-2], widened[:, :, 2:])
    coupled = jnp.zeros(psi.shape, jnp.float32)
    for face in range(4):
        coupled = coupled + jnp.einsum(
            "abij,bij->aij",
            face_jacobian[face].astype(jnp.float32),
            sides[face],
            precision=lax.Precision.HIGHEST,
        )
    return coupled


def body(
    right_side,
    adjoint_start,
    diag_inverse,
    face_jacobian,
    receptor_cell,
    donor_cell,
    donor_weight,
    live_count,
):
    nvar, rows, cols = right_side.shape
    cells = rows * cols
    slots = receptor_cell.shape[2]
    live = (jnp.arange(slots, dtype=jnp.int32)[None, :] < live_count[0][:, None]).astype(
        jnp.float32
    )
    targets = lax.all_to_all(donor_cell[0], "blk", split_axis=0, concat_axis=0, tiled=True).reshape(
        -1
    )
    sources = receptor_cell[0].reshape(-1)
    rhs_local = jnp.sum(right_side * right_side)
    psi = adjoint_start
    partials = []
    for sweep in range(SWEEPS):
        picked = pick_cells(psi.reshape(nvar, cells), sources, slots)
        values = picked.reshape(nvar, -1, slots) * live[None]
        weighted = values[:, :, None, :] * donor_weight[0][None]
        terms = lax.all_to_all(weighted, "blk", split_axis=1, concat_axis=1, tiled=True)
        spread = spread_cells(terms.reshape(nvar, -1), targets, cells, 4 * slots)
        coupled = face_coupling(psi, face_jacobian)
        source = right_side - coupled + spread.reshape(psi.shape)
        new = jnp.einsum("abij,bij->aij", diag_inverse, source, precision=lax.Precision.HIGHEST)
        change = new - psi
        partial_sq = jnp.sum(change * change)
        partials.append(partial_sq)
        psi = new
    totals = lax.psum(jnp.stack([rhs_local] + partials), "blk")
    result_norms = jnp.sqrt(totals[1:] / (totals[0] + 1e-06))
    return (psi, result_norms)


def solution(mesh):
    return jax.shard_map(
        body,
        mesh=mesh,
        in_specs=(
            P(None, ("design", "blk"), None),
            P(None, ("design", "blk"), None),
            P(None, None, ("design", "blk"), None),
            P(None, None, None, ("design", "blk"), None),
            P(("design", "blk"), None, None),
            P(("design", "blk"), None, None, None),
            P(("design", "blk"), None, None, None),
            P(("design", "blk"), None),
        ),
        out_specs=(P(None, ("design", "blk"), None), P("design")),
        check_vma=False,
    )
```

profile of v0, /device:TPU:0, one launch (start us, length us, event | category | flops | bytes accessed | tf_op | source)
XLA Modules:
  0.0 102.9 jit_solution(15937769331518278682)
XLA Ops:
  0.6 0.0 copy-start.4
  0.6 0.0 copy-start.12
  0.7 7.6 %all-to-all-start.1 = ((s32[16,4,16]{2,1,0:T(4,128)}), s32[16,4,16]{2,1,0:T(4,128)S(1)}, u32[]{:S(2)}, u32[]{:S(2)}) async-start(s32[16,4,16]{2,1,0:T(4,128)} %bitcast.113), calls=%async_computation.1 | async-start | bytes 65536 | tf_op jit(solution)/shard_map/all_to_all | solution.py:110
  8.2 1.1 %fusion.46 = (f32[6,1,1024]{2,1,0:T(1,128)S(1)}, f32[6,1,1024]{2,1,0:T(1,128)S(1)}) fusion(f32[6,8,1024]{2,1,0:T(8,128)} %param.9), kind=kLoop, calls=%fused_computation.89 | loop fusion | bytes 98304 | tf_op jit(solution)/shard_map/slice | solution.py:16
  9.3 2.3 %collective-permute-start = (f32[6,1,1024]{2,1,0:T(1,128)S(1)}, f32[6,1,1024]{2,1,0:T(1,128)S(1)}, u32[]{:S(2)}, u32[]{:S(2)}) collective-permute-start(f32[6,1,1024]{2,1,0:T(1,128)S(1)} %get-tuple-element.74), channel_id=1, source_target_pairs={{0,1},{1,2},{2,3},{3,4},{4,5},{5,6},{6,7},{7,8},{8,9},{9,10},{10,1... | collective-permute-start | bytes 73736 | tf_op jit(solution)/shard_map/ppermute | solution.py:15
  11.6 1.3 %collective-permute-start.1 = (f32[6,1,1024]{2,1,0:T(1,128)S(1)}, f32[6,1,1024]{2,1,0:T(1,128)S(1)}, u32[]{:S(2)}, u32[]{:S(2)}) collective-permute-start(f32[6,1,1024]{2,1,0:T(1,128)S(1)} %get-tuple-element.75), channel_id=1, source_target_pairs={{1,0},{2,1},{3,2},{4,3},{5,4},{6,5},{7,6},{8,7},{9,8},{10,9},{11,1... | collective-permute-start | bytes 73736 | tf_op jit(solution)/shard_map/ppermute | solution.py:18
  12.9 1.0 reshape_reshape.20
  13.9 0.8 squeeze.43
  14.7 0.0 copy-start.16
  14.7 0.7 fusion.42
  15.4 0.0 copy-start
  15.4 0.5 fusion.4
  16.0 0.1 copy-done.13
  16.1 0.1 reshape_reshape.21
  16.2 0.8 reshape.189
  17.0 0.0 all-to-all-done.1
  17.0 8.0 %all-to-all-start = ((f32[16,1,384]{2,1,0:T(1,128)}), f32[16,1,384]{2,1,0:T(1,128)S(1)}, u32[]{:S(2)}, u32[]{:S(2)}) async-start(f32[16,1,384]{2,1,0:T(1,128)} %reshape.189), calls=%async_computation | async-start | bytes 49152 | tf_op jit(solution)/shard_map/all_to_all | solution.py:121
  25.0 0.1 squeeze.45
  25.1 0.7 fusion.23
  25.8 0.0 collective-permute-done
  25.8 0.0 collective-permute-done.1
  25.8 0.2 fusion.24
  26.0 1.4 %fusion.8 = (f32[8,1024,6]{1,0,2:T(8,128)}, f32[8,1024,6]{1,0,2:T(8,128)}, f32[8,1024,6]{1,0,2:T(8,128)}, f32[8,1024,6]{1,0,2:T(8,128)}) fusion(f32[8,1024,6]{1,0,2:T(8,128)S(1)} %get-tuple-element.73, bf16[4,6,6,8,1024]{4,3,2,1,0:T(8,128)(2,1)S(1)} %copy-done, f32[8,1024,6]{1,0,2:T(8,128)S(1)} %get-tuple-element.72, ...), kind=kLoop, calls=%fused_computation.18 | loop fusion | flops 3342336 | bytes 3932160 | tf_op jit(solution)/shard_map/abij,bij->aij/dot_general | solution.py:85
  27.5 4.1 %all-to-all-done = f32[16,1,384]{2,1,0:T(1,128)S(1)} async-done(((f32[16,1,384]{2,1,0:T(1,128)}), f32[16,1,384]{2,1,0:T(1,128)S(1)}, u32[]{:S(2)}, u32[]{:S(2)}) %all-to-all-start) | async-done | bytes 24608 | tf_op jit(solution)/shard_map/all_to_all | solution.py:121
  31.6 0.5 broadcast.186
  32.1 0.7 reduce.20
  32.8 0.2 reshape.190
  33.0 0.8 mul.150
  33.8 2.7 %fusion.2 = f32[6,64,128]{2,1,0:T(8,128)} fusion(f32[1024,64]{0,1:T(8,128)} %fusion.23, f32[6,1024]{1,0:T(8,128)} %mul.150, s32[1024]{0:T(1024)S(1)} %get-tuple-element.76), kind=kOutput, calls=%fused_computation.2 | convolution fusion | flops 604504064 | bytes 487424 | tf_op jit(solution)/shard_map/while/body/eval_jaxpr/atb,to->abo/dot_general | solution.py:71
  36.5 1.6 %reshape_reshape.22 = f32[6,8,1024]{2,1,0:T(8,128)} reshape(f32[6,64,128]{2,1,0:T(8,128)} %fusion.2) | data formatting | bytes 393216 | tf_op jit(solution)/shard_map/reshape;reshape | solution.py:124
  38.2 2.0 %multiply_reduce_fusion.4 = (f32[]{:T(128)}, f32[8,1024,6]{1,0,2:T(8,128)S(1)}) fusion(f32[6,8,1024]{2,1,0:T(8,128)} %param.8, f32[6,8,1024]{2,1,0:T(8,128)} %reshape_reshape.22, f32[8,1024,6]{1,0,2:T(8,128)} %get-tuple-element.48, f32[8,1024,6]{1,0,2:T(8,128)} %get-tuple-element.49, f32[8,1024,6]{1,0,2:T(8,128)} %get-tuple-element.43, ...), kind=kLoop, calls=%fused_computation.60 | loop fusion | flops 344063 | bytes 1376260 | tf_op jit(solution)/shard_map/reduce_sum | solution.py:114
  40.1 0.1 multiply_reduce_fusion.1
  40.3 0.0 copy-start.2
  40.3 0.7 copy-done.2
  40.9 0.6 fusion.45
  41.6 1.6 %reshape_reshape.23 = f32[6,64,128]{2,1,0:T(8,128)} reshape(f32[6,8,1024]{2,1,0:T(8,128)} %bitcast.106) | data formatting | bytes 393216 | tf_op jit(solution)/shard_map/reshape;reshape | solution.py:44
  43.2 2.2 %collective-permute-start.2 = (f32[6,1,1024]{2,1,0:T(1,128)}, f32[6,1,1024]{2,1,0:T(1,128)}, u32[]{:S(2)}, u32[]{:S(2)}) collective-permute-start(f32[6,1,1024]{2,1,0:T(1,128)} %get-tuple-element.68), channel_id=1, source_target_pairs={{0,1},{1,2},{2,3},{3,4},{4,5},{5,6},{6,7},{7,8},{8,9},{9,10},{10,1... | collective-permute-start | bytes 73736 | tf_op jit(solution)/shard_map/ppermute | solution.py:15
  45.4 1.3 %collective-permute-start.3 = (f32[6,1,1024]{2,1,0:T(1,128)}, f32[6,1,1024]{2,1,0:T(1,128)}, u32[]{:S(2)}, u32[]{:S(2)}) collective-permute-start(f32[6,1,1024]{2,1,0:T(1,128)} %get-tuple-element.69), channel_id=1, source_target_pairs={{1,0},{2,1},{3,2},{4,3},{5,4},{6,5},{7,6},{8,7},{9,8},{10,9},{11,1... | collective-permute-start | bytes 73736 | tf_op jit(solution)/shard_map/ppermute | solution.py:18
  46.7 1.5 %fusion.5 = f32[256,6]{0,1:T(8,128)S(1)} fusion(f32[6,64,128]{2,1,0:T(8,128)} %reshape_reshape.23, f32[256,128]{0,1:T(8,128)} %copy-done.13, s32[256]{0:T(256)} %copy-done.16), kind=kOutput, calls=%fused_computation.15 | convolution fusion | flops 151403008 | bytes 334848 | tf_op jit(solution)/shard_map/while/body/eval_jaxpr/tb,abo->tao/dot_general | solution.py:50
  48.3 0.7 reshape_reshape.24
  49.0 0.8 broadcast_multiply_fusion.2
  49.8 1.5 %fusion.48 = f32[16,6,4,16]{3,2,1,0:T(4,128)} fusion(f32[16,4,16]{2,1,0:T(4,128)} %bitcast.111, f32[6,16,16]{2,0,1:T(8,128)S(1)} %copy.14), kind=kLoop, calls=%fused_computation.91 | loop fusion | flops 6144 | bytes 34816
  51.3 1.7 %reshape.191 = f32[16,1,384]{2,1,0:T(1,128)} reshape(f32[16,6,4,16]{3,2,1,0:T(4,128)} %fusion.48) | data formatting | bytes 49152
  53.0 4.9 %all-to-all-start.2 = ((f32[16,1,384]{2,1,0:T(1,128)}), f32[16,1,384]{2,1,0:T(1,128)}, u32[]{:S(2)}, u32[]{:S(2)}) async-start(f32[16,1,384]{2,1,0:T(1,128)} %reshape.191), calls=%async_computation.2 | async-start | bytes 49152 | tf_op jit(solution)/shard_map/all_to_all | solution.py:121
  57.9 0.0 collective-permute-done.2
  57.9 0.0 collective-permute-done.3
  57.9 1.4 %fusion.27 = (f32[8,1024,6]{1,0,2:T(8,128)S(1)}, f32[8,1024,6]{1,0,2:T(8,128)S(1)}, f32[8,1024,6]{1,0,2:T(8,128)S(1)}, f32[8,1024,6]{1,0,2:T(8,128)S(1)}) fusion(f32[6,8,1024]{2,1,0:T(8,128)} %bitcast.107, f32[6,1,1024]{2,1,0:T(1,128)} %collective-permute-done.2, f32[6,1,1024]{2,1,0:T(1,128)} %collective-permute-done.3), kind=kLoop, calls=%fused_computation.43 | loop fusion | flops 98304 | bytes 1032192
  59.3 1.4 %fusion.9 = (f32[8,1024,6]{1,0,2:T(8,128)}, f32[8,1024,6]{1,0,2:T(8,128)}, f32[8,1024,6]{1,0,2:T(8,128)}, f32[8,1024,6]{1,0,2:T(8,128)}) fusion(f32[8,1024,6]{1,0,2:T(8,128)S(1)} %get-tuple-element.67, bf16[4,6,6,8,1024]{4,3,2,1,0:T(8,128)(2,1)S(1)} %copy-done, f32[8,1024,6]{1,0,2:T(8,128)S(1)} %get-tuple-element.66, ...), kind=kLoop, calls=%fused_computation.19 | loop fusion | flops 3342336 | bytes 3932160 | tf_op jit(solution)/shard_map/abij,bij->aij/dot_general | solution.py:85
  60.8 3.7 %all-to-all-done.2 = f32[16,1,384]{2,1,0:T(1,128)} async-done(((f32[16,1,384]{2,1,0:T(1,128)}), f32[16,1,384]{2,1,0:T(1,128)}, u32[]{:S(2)}, u32[]{:S(2)}) %all-to-all-start.2) | async-done | bytes 24608 | tf_op jit(solution)/shard_map/all_to_all | solution.py:121
  64.5 1.4 %reduce.21 = f32[16,384]{1,0:T(8,128)S(1)} reduce(f32[16,1,384]{2,1,0:T(1,128)} %all-to-all-done.2, f32[]{:T(128)} %broadcast.186), dimensions={1}, to_apply=%all_to_all.11.reduce_sub_computation | reduce | bytes 49156 | tf_op jit(solution)/shard_map/all_to_all | solution.py:121
  66.0 0.2 reshape.192
  66.2 0.2 mul.159
  66.4 1.9 %fusion = f32[6,64,128]{2,1,0:T(8,128)S(1)} fusion(f32[6,1024]{1,0:T(8,128)S(1)} %mul.159, f32[1024,64]{0,1:T(8,128)} %fusion.23, s32[1024]{0:T(1024)S(1)} %copy-done.15), kind=kOutput, calls=%fused_computation | convolution fusion | flops 604504064 | bytes 487424 | tf_op jit(solution)/shard_map/while/body/eval_jaxpr/atb,to->abo/dot_general | solution.py:71
  68.4 0.0 copy-done.7
  68.4 0.0 copy-start.3
  68.4 0.0 copy-start.5
  68.4 0.1 fusion.33
  68.5 0.1 multiply_reduce_fusion
  68.6 0.7 copy-done.3
  69.3 0.1 copy-done.5
  69.4 0.8 multiply_reduce_fusion.3
  70.2 2.0 %pad_maximum_fusion.4 = f32[3]{0:T(128)S(1)} fusion(f32[1]{0:T(128)} %bitcast.49, f32[1]{0:T(128)} %bitcast.48, f32[1]{0:T(128)} %bitcast.47), kind=kLoop, calls=%fused_computation.86 | loop fusion | flops 6 | bytes 24 | tf_op jit(solution)/shard_map/stack | solution.py:130
  72.1 30.1 %psum.7 = f32[3]{0:T(128)S(1)} all-reduce(f32[3]{0:T(128)S(1)} %pad_maximum_fusion.4), channel_id=1, replica_groups=mesh['design'=2,'blk'=16] {'blk'}, use_global_device_ids=true, to_apply=%region_5.6 | all-reduce | flops 3 | bytes 24 | tf_op jit(solution)/shard_map/psum | solution.py:130
  102.3 0.6 divide_sqrt_fusion
  (32 shorter events, 0.3 us)
Async XLA Ops:
  0.6 25.2 %copy-start.4 = (f32[6,8,1024]{2,1,0:T(8,128)S(1)}, f32[6,8,1024]{2,1,0:T(8,128)}, u32[]{:S(2)}) copy-start(f32[6,8,1024]{2,1,0:T(8,128)} %param.9) | copy-start | bytes 589828
  0.6 15.5 %copy-start.12 = (f32[1,16,4,16]{3,2,1,0:T(4,128)S(1)}, f32[1,16,4,16]{3,2,1,0:T(4,128)}, u32[]{:S(2)}) copy-start(f32[1,16,4,16]{3,2,1,0:T(4,128)} %param.14) | copy-start | bytes 12292
  0.7 16.4 %all-to-all-start.1 = ((s32[16,4,16]{2,1,0:T(4,128)}), s32[16,4,16]{2,1,0:T(4,128)S(1)}, u32[]{:S(2)}, u32[]{:S(2)}) async-start(s32[16,4,16]{2,1,0:T(4,128)} %bitcast.113), calls=%async_computation.1 | async-start | bytes 65536 | tf_op jit(solution)/shard_map/all_to_all | solution.py:110
  9.3 16.5 %collective-permute-start = (f32[6,1,1024]{2,1,0:T(1,128)S(1)}, f32[6,1,1024]{2,1,0:T(1,128)S(1)}, u32[]{:S(2)}, u32[]{:S(2)}) collective-permute-start(f32[6,1,1024]{2,1,0:T(1,128)S(1)} %get-tuple-element.74), channel_id=1, source_target_pairs={{0,1},{1,2},{2,3},{3,4},{4,5},{5,6},{6,7},{7,8},{8,9},{9,10},{10,1... | collective-permute-start | bytes 73736 | tf_op jit(solution)/shard_map/ppermute | solution.py:15
  11.6 14.2 %collective-permute-start.1 = (f32[6,1,1024]{2,1,0:T(1,128)S(1)}, f32[6,1,1024]{2,1,0:T(1,128)S(1)}, u32[]{:S(2)}, u32[]{:S(2)}) collective-permute-start(f32[6,1,1024]{2,1,0:T(1,128)S(1)} %get-tuple-element.75), channel_id=1, source_target_pairs={{1,0},{2,1},{3,2},{4,3},{5,4},{6,5},{7,6},{8,7},{9,8},{10,9},{11,1... | collective-permute-start | bytes 73736 | tf_op jit(solution)/shard_map/ppermute | solution.py:18
  14.7 11.4 %copy-start.16 = (s32[256]{0:T(256)}, s32[256]{0:T(256)S(1)}, u32[]{:S(2)}) copy-start(s32[256]{0:T(256)S(1)} %get-tuple-element.57) | copy-start | bytes 3076
  15.4 0.6 copy-start.13
  15.4 10.6 %copy-start = (bf16[4,6,6,8,1024]{4,3,2,1,0:T(8,128)(2,1)S(1)}, bf16[4,6,6,8,1024]{4,3,2,1,0:T(8,128)(2,1)}, u32[]{:S(2)}) copy-start(bf16[4,6,6,8,1024]{4,3,2,1,0:T(8,128)(2,1)} %param.11) | copy-start | bytes 7077892
  17.0 14.5 %all-to-all-start = ((f32[16,1,384]{2,1,0:T(1,128)}), f32[16,1,384]{2,1,0:T(1,128)S(1)}, u32[]{:S(2)}, u32[]{:S(2)}) async-start(f32[16,1,384]{2,1,0:T(1,128)} %reshape.189), calls=%async_computation | async-start | bytes 49152 | tf_op jit(solution)/shard_map/all_to_all | solution.py:121
  25.1 8.7 %copy-start.14 = (s32[1024]{0:T(1024)}, s32[1024]{0:T(1024)S(1)}, u32[]{:S(2)}) copy-start(s32[1024]{0:T(1024)S(1)} %get-tuple-element.76) | copy-start | bytes 12292
  33.8 6.3 %copy-start.1 = (f32[6,6,8,1024]{3,2,1,0:T(8,128)S(1)}, f32[6,6,8,1024]{3,2,1,0:T(8,128)}, u32[]{:S(2)}) copy-start(f32[6,6,8,1024]{3,2,1,0:T(8,128)} %param.10) | copy-start | bytes 3538948
  40.3 0.7 copy-start.2
  43.2 14.7 %collective-permute-start.2 = (f32[6,1,1024]{2,1,0:T(1,128)}, f32[6,1,1024]{2,1,0:T(1,128)}, u32[]{:S(2)}, u32[]{:S(2)}) collective-permute-start(f32[6,1,1024]{2,1,0:T(1,128)} %get-tuple-element.68), channel_id=1, source_target_pairs={{0,1},{1,2},{2,3},{3,4},{4,5},{5,6},{6,7},{7,8},{8,9},{9,10},{10,1... | collective-permute-start | bytes 73736 | tf_op jit(solution)/shard_map/ppermute | solution.py:15
  45.4 12.5 %collective-permute-start.3 = (f32[6,1,1024]{2,1,0:T(1,128)}, f32[6,1,1024]{2,1,0:T(1,128)}, u32[]{:S(2)}, u32[]{:S(2)}) collective-permute-start(f32[6,1,1024]{2,1,0:T(1,128)} %get-tuple-element.69), channel_id=1, source_target_pairs={{1,0},{2,1},{3,2},{4,3},{5,4},{6,5},{7,6},{8,7},{9,8},{10,9},{11,1... | collective-permute-start | bytes 73736 | tf_op jit(solution)/shard_map/ppermute | solution.py:18
  53.0 11.5 %all-to-all-start.2 = ((f32[16,1,384]{2,1,0:T(1,128)}), f32[16,1,384]{2,1,0:T(1,128)}, u32[]{:S(2)}, u32[]{:S(2)}) async-start(f32[16,1,384]{2,1,0:T(1,128)} %reshape.191), calls=%async_computation.2 | async-start | bytes 49152 | tf_op jit(solution)/shard_map/all_to_all | solution.py:121
  59.3 7.0 %copy-start.15 = (s32[1024]{0:T(1024)S(1)}, s32[1024]{0:T(1024)}, u32[]{:S(2)}) copy-start(s32[1024]{0:T(1024)} %copy-done.14) | copy-start | bytes 12292
  60.8 7.6 %copy-start.7 = (f32[6,8,1024]{2,1,0:T(8,128)S(1)}, f32[6,8,1024]{2,1,0:T(8,128)}, u32[]{:S(2)}) copy-start(f32[6,8,1024]{2,1,0:T(8,128)} %param.8) | copy-start | bytes 589828
  60.8 7.6 %copy-start.8 = (f32[8,1024,6]{1,0,2:T(8,128)S(1)}, f32[8,1024,6]{1,0,2:T(8,128)}, u32[]{:S(2)}) copy-start(f32[8,1024,6]{1,0,2:T(8,128)} %get-tuple-element.34) | copy-start | bytes 589828
  60.8 7.6 %copy-start.9 = (f32[8,1024,6]{1,0,2:T(8,128)S(1)}, f32[8,1024,6]{1,0,2:T(8,128)}, u32[]{:S(2)}) copy-start(f32[8,1024,6]{1,0,2:T(8,128)} %get-tuple-element.35) | copy-start | bytes 589828
  60.8 7.6 %copy-start.10 = (f32[8,1024,6]{1,0,2:T(8,128)S(1)}, f32[8,1024,6]{1,0,2:T(8,128)}, u32[]{:S(2)}) copy-start(f32[8,1024,6]{1,0,2:T(8,128)} %get-tuple-element.40) | copy-start | bytes 589828
  60.8 7.6 %copy-start.11 = (f32[8,1024,6]{1,0,2:T(8,128)S(1)}, f32[8,1024,6]{1,0,2:T(8,128)}, u32[]{:S(2)}) copy-start(f32[8,1024,6]{1,0,2:T(8,128)} %get-tuple-element.41) | copy-start | bytes 589828
  68.4 0.9 copy-start.3
  68.4 1.0 copy-start.5
  69.4 33.5 %copy-start.6 = (f32[8,1024,6]{1,0,2:T(8,128)}, f32[8,1024,6]{1,0,2:T(8,128)S(1)}, u32[]{:S(2)}) copy-start(f32[8,1024,6]{1,0,2:T(8,128)S(1)} %multiply_reduce_fusion) | copy-start | bytes 589828
where the time goes:
time: 104 us; the launch traced here: 103 us
  blocking collectives  30.1 us (29%)
  starting transfers between devices  27.5 us (26%)
  other arithmetic  16 us (15%)
  local copies, waits for them, and re-layouts  13.7 us (13%)
  waiting for transfers between devices  7.82 us (8%)
  matrix products  6.72 us (6%)
  between operations  1.06 us (1%)
    psum x1, blocking collectives, body(): totals = lax.psum(jnp.stack([rhs_local] + partials), 'blk')  30.1 us
    all_to_all x2, starting transfers between devices, body(): lax.all_to_all(weighted, 'blk', split_axis=1, concat_axis=1, tiled=True)  12.9 us
    all_to_all x2, waiting for transfers between devices, body(): lax.all_to_all(weighted, 'blk', split_axis=1, concat_axis=1, tiled=True)  7.81 us
    all_to_all x1, starting transfers between devices, body(): lax.all_to_all(donor_cell[0], 'blk', split_axis=0, concat_axis=0, tiled=T...  7.56 us
    dot_general x2, matrix products, spread_one_group(): jnp.einsum('atb,to->abo', weighted, offset_hot, precision=lax.Precision.H...  4.65 us
    ppermute x2, starting transfers between devices, padded_2(): lax.ppermute(lax.slice_in_dim(block, block.shape[dim] - width, None, axis...  4.52 us
    unnamed x38, local copies, waits for them, and re-layouts  4.45 us
    unnamed x5, other arithmetic  3.18 us
  transfers between devices with their start and end apart: 7, of which 2 were waited for; matrix products, arithmetic and copies ran while one was open for 16% of the time, Pallas kernels for 0%

commit v1 on v0

--- a/solution.py
+++ b/solution.py
@@ -5,6 +5,7 @@
 from jax.sharding import PartitionSpec as P
 
 SWEEPS = 2
+_hold_pairs_all = lambda raw: lax.all_gather(raw, "blk").sum(axis=0)
 
 
 def padded_2(block, sides, width):
@@ -127,7 +128,7 @@
         partial_sq = jnp.sum(change * change)
         partials.append(partial_sq)
         psi = new
-    totals = lax.psum(jnp.stack([rhs_local] + partials), "blk")
+    totals = _hold_pairs_all(jnp.stack([rhs_local] + partials))
     result_norms = jnp.sqrt(totals[1:] / (totals[0] + 1e-06))
     return (psi, result_norms)
 

time: 104 us -> 107 us (1.029)
  other arithmetic: 16 us -> 17.1 us
    unnamed x0 -> x1, blocking collectives: none -> 30.1 us
    psum x1 -> x0, blocking collectives: 30.1 us -> none  [body(): totals = lax.psum(jnp.stack([rhs_local] + partials), 'blk')]
    unnamed x5 -> x6, other arithmetic: 3.18 us -> 5.35 us
    another operation x1 -> x0, other arithmetic: 1.95 us -> none  [body(): totals = lax.psum(jnp.stack([rhs_local] + partials), 'blk')]
    unnamed x38 -> x40, local copies, waits for them, and re-layouts: 4.45 us -> 4.35 us
  transfers between devices with their start and end apart: 7 -> 7, of which waited for: 2 -> 2; matrix products, arithmetic and copies ran while one was open for 16% -> 13% of each run, Pallas kernels for 0% -> 0%
where the time goes in v1:
time: 107 us; the launch traced here: 106 us
  blocking collectives  30.1 us (28%)
  starting transfers between devices  27.5 us (26%)
  other arithmetic  17.1 us (16%)
  local copies, waits for them, and re-layouts  14.7 us (14%)
  waiting for transfers between devices  7.83 us (7%)
  matrix products  6.73 us (6%)
  between operations  1.74 us (2%)
    unnamed x1, blocking collectives  30.1 us
    all_to_all x2, starting transfers between devices, body(): lax.all_to_all(weighted, 'blk', split_axis=1, concat_axis=1, tiled=True)  12.9 us
    all_to_all x2, waiting for transfers between devices, body(): lax.all_to_all(weighted, 'blk', split_axis=1, concat_axis=1, tiled=True)  7.82 us
    all_to_all x1, starting transfers between devices, body(): lax.all_to_all(donor_cell[0], 'blk', split_axis=0, concat_axis=0, tiled=T...  7.56 us
    unnamed x6, other arithmetic  5.35 us
    dot_general x2, matrix products, spread_one_group(): jnp.einsum('atb,to->abo', weighted, offset_hot, precision=lax.Precision.H...  4.65 us
    ppermute x2, starting transfers between devices, padded_2(): lax.ppermute(lax.slice_in_dim(block, block.shape[dim] - width, None, axis...  4.53 us
    unnamed x40, local copies, waits for them, and re-layouts  4.35 us
  transfers between devices with their start and end apart: 7, of which 2 were waited for; matrix products, arithmetic and copies ran while one was open for 13% of the time, Pallas kernels for 0%

profile of v1, /device:TPU:0, one launch (start us, length us, event | category | flops | bytes accessed | tf_op | source)
XLA Modules:
  0.0 105.7 jit_solution(4198142137280219755)
XLA Ops:
  0.6 0.0 copy-start.16
  0.6 0.0 copy-start.3
  0.7 0.0 copy-start.11
  0.7 7.6 %all-to-all-start.1 = ((s32[16,4,16]{2,1,0:T(4,128)}), s32[16,4,16]{2,1,0:T(4,128)S(1)}, u32[]{:S(2)}, u32[]{:S(2)}) async-start(s32[16,4,16]{2,1,0:T(4,128)} %bitcast.114), calls=%async_computation.1 | async-start | bytes 65536 | tf_op jit(solution)/shard_map/all_to_all | solution.py:111
  8.2 1.1 %fusion.46 = (f32[6,1,1024]{2,1,0:T(1,128)S(1)}, f32[6,1,1024]{2,1,0:T(1,128)S(1)}) fusion(f32[6,8,1024]{2,1,0:T(8,128)} %param.9), kind=kLoop, calls=%fused_computation.89 | loop fusion | bytes 98304 | tf_op jit(solution)/shard_map/slice | solution.py:17
  9.3 2.3 %collective-permute-start = (f32[6,1,1024]{2,1,0:T(1,128)S(1)}, f32[6,1,1024]{2,1,0:T(1,128)S(1)}, u32[]{:S(2)}, u32[]{:S(2)}) collective-permute-start(f32[6,1,1024]{2,1,0:T(1,128)S(1)} %get-tuple-element.74), channel_id=1, source_target_pairs={{0,1},{1,2},{2,3},{3,4},{4,5},{5,6},{6,7},{7,8},{8,9},{9,10},{10,1... | collective-permute-start | bytes 73736 | tf_op jit(solution)/shard_map/ppermute | solution.py:16
  11.6 1.3 %collective-permute-start.1 = (f32[6,1,1024]{2,1,0:T(1,128)S(1)}, f32[6,1,1024]{2,1,0:T(1,128)S(1)}, u32[]{:S(2)}, u32[]{:S(2)}) collective-permute-start(f32[6,1,1024]{2,1,0:T(1,128)S(1)} %get-tuple-element.75), channel_id=1, source_target_pairs={{1,0},{2,1},{3,2},{4,3},{5,4},{6,5},{7,6},{8,7},{9,8},{10,9},{11,1... | collective-permute-start | bytes 73736 | tf_op jit(solution)/shard_map/ppermute | solution.py:19
  12.9 1.0 reshape_reshape.20
  13.9 0.8 squeeze.43
  14.7 0.0 copy-start.12
  14.7 0.0 copy-start
  14.7 0.5 fusion.4
  15.3 0.1 copy-done.12
  15.3 0.1 reshape_reshape.21
  15.4 0.8 fusion.42
  16.3 0.8 reshape.195
  17.1 0.6 dynamic-slice
  18.3 0.0 all-to-all-done.1
  18.3 8.0 %all-to-all-start = ((f32[16,1,384]{2,1,0:T(1,128)}), f32[16,1,384]{2,1,0:T(1,128)S(1)}, u32[]{:S(2)}, u32[]{:S(2)}) async-start(f32[16,1,384]{2,1,0:T(1,128)} %reshape.195), calls=%async_computation | async-start | bytes 49152 | tf_op jit(solution)/shard_map/all_to_all | solution.py:122
  26.3 0.1 squeeze.45
  26.4 0.7 fusion.23
  27.1 0.0 collective-permute-done
  27.2 0.0 collective-permute-done.1
  27.2 0.2 fusion.24
  27.4 1.4 %fusion.8 = (f32[8,1024,6]{1,0,2:T(8,128)}, f32[8,1024,6]{1,0,2:T(8,128)}, f32[8,1024,6]{1,0,2:T(8,128)}, f32[8,1024,6]{1,0,2:T(8,128)}) fusion(f32[8,1024,6]{1,0,2:T(8,128)S(1)} %get-tuple-element.73, bf16[4,6,6,8,1024]{4,3,2,1,0:T(8,128)(2,1)S(1)} %copy-done, f32[8,1024,6]{1,0,2:T(8,128)S(1)} %get-tuple-element.72, ...), kind=kLoop, calls=%fused_computation.18 | loop fusion | flops 3342336 | bytes 3932160 | tf_op jit(solution)/shard_map/abij,bij->aij/dot_general | solution.py:86
  28.8 4.1 %all-to-all-done = f32[16,1,384]{2,1,0:T(1,128)S(1)} async-done(((f32[16,1,384]{2,1,0:T(1,128)}), f32[16,1,384]{2,1,0:T(1,128)S(1)}, u32[]{:S(2)}, u32[]{:S(2)}) %all-to-all-start) | async-done | bytes 24608 | tf_op jit(solution)/shard_map/all_to_all | solution.py:122
  32.9 0.5 broadcast.187
  33.4 0.7 reduce.20
  34.1 0.2 reshape.196
  34.3 0.8 mul.150
  35.1 2.7 %fusion.2 = f32[6,64,128]{2,1,0:T(8,128)} fusion(f32[1024,64]{0,1:T(8,128)} %fusion.23, f32[6,1024]{1,0:T(8,128)} %mul.150, s32[1024]{0:T(1024)S(1)} %get-tuple-element.76), kind=kOutput, calls=%fused_computation.2 | convolution fusion | flops 604504064 | bytes 487424 | tf_op jit(solution)/shard_map/while/body/eval_jaxpr/atb,to->abo/dot_general | solution.py:72
  37.8 1.6 %reshape_reshape.22 = f32[6,8,1024]{2,1,0:T(8,128)} reshape(f32[6,64,128]{2,1,0:T(8,128)} %fusion.2) | data formatting | bytes 393216 | tf_op jit(solution)/shard_map/reshape;reshape | solution.py:125
  39.5 2.1 %multiply_reduce_fusion.4 = (f32[]{:T(128)}, f32[8,1024,6]{1,0,2:T(8,128)S(1)}) fusion(f32[6,8,1024]{2,1,0:T(8,128)} %param.8, f32[6,8,1024]{2,1,0:T(8,128)} %reshape_reshape.22, f32[8,1024,6]{1,0,2:T(8,128)} %get-tuple-element.48, f32[8,1024,6]{1,0,2:T(8,128)} %get-tuple-element.49, f32[8,1024,6]{1,0,2:T(8,128)} %get-tuple-element.43, ...), kind=kLoop, calls=%fused_computation.60 | loop fusion | flops 344063 | bytes 1376260 | tf_op jit(solution)/shard_map/reduce_sum | solution.py:115
  41.6 0.8 multiply_reduce_fusion.1
  42.3 1.6 %reshape_reshape.23 = f32[6,64,128]{2,1,0:T(8,128)} reshape(f32[6,8,1024]{2,1,0:T(8,128)} %bitcast.106) | data formatting | bytes 393216 | tf_op jit(solution)/shard_map/reshape;reshape | solution.py:45
  44.0 1.7 %fusion.45 = (f32[6,1,1024]{2,1,0:T(1,128)}, f32[6,1,1024]{2,1,0:T(1,128)}) fusion(f32[6,8,1024]{2,1,0:T(8,128)} %bitcast.107), kind=kLoop, calls=%fused_computation.88 | loop fusion | bytes 98304 | tf_op jit(solution)/shard_map/slice | solution.py:17
  45.7 1.5 %fusion.5 = f32[256,6]{0,1:T(8,128)S(1)} fusion(f32[6,64,128]{2,1,0:T(8,128)} %reshape_reshape.23, f32[256,128]{0,1:T(8,128)} %copy-done.12, s32[256]{0:T(256)} %copy-done.15), kind=kOutput, calls=%fused_computation.15 | convolution fusion | flops 151403008 | bytes 334848 | tf_op jit(solution)/shard_map/while/body/eval_jaxpr/tb,abo->tao/dot_general | solution.py:51
  47.2 0.7 reshape_reshape.24
  47.9 0.8 broadcast_multiply_fusion.2
  48.7 2.2 %collective-permute-start.2 = (f32[6,1,1024]{2,1,0:T(1,128)}, f32[6,1,1024]{2,1,0:T(1,128)}, u32[]{:S(2)}, u32[]{:S(2)}) collective-permute-start(f32[6,1,1024]{2,1,0:T(1,128)} %get-tuple-element.68), channel_id=1, source_target_pairs={{0,1},{1,2},{2,3},{3,4},{4,5},{5,6},{6,7},{7,8},{8,9},{9,10},{10,1... | collective-permute-start | bytes 73736 | tf_op jit(solution)/shard_map/ppermute | solution.py:16
  50.9 1.3 %collective-permute-start.3 = (f32[6,1,1024]{2,1,0:T(1,128)}, f32[6,1,1024]{2,1,0:T(1,128)}, u32[]{:S(2)}, u32[]{:S(2)}) collective-permute-start(f32[6,1,1024]{2,1,0:T(1,128)} %get-tuple-element.69), channel_id=1, source_target_pairs={{1,0},{2,1},{3,2},{4,3},{5,4},{6,5},{7,6},{8,7},{9,8},{10,9},{11,1... | collective-permute-start | bytes 73736 | tf_op jit(solution)/shard_map/ppermute | solution.py:19
  52.2 1.5 %fusion.48 = f32[16,6,4,16]{3,2,1,0:T(4,128)} fusion(f32[16,4,16]{2,1,0:T(4,128)} %bitcast.112, f32[6,16,16]{2,0,1:T(8,128)S(1)} %copy.14), kind=kLoop, calls=%fused_computation.91 | loop fusion | flops 6144 | bytes 34816
  53.7 1.7 %reshape.197 = f32[16,1,384]{2,1,0:T(1,128)} reshape(f32[16,6,4,16]{3,2,1,0:T(4,128)} %fusion.48) | data formatting | bytes 49152
  55.4 4.9 %all-to-all-start.2 = ((f32[16,1,384]{2,1,0:T(1,128)}), f32[16,1,384]{2,1,0:T(1,128)}, u32[]{:S(2)}, u32[]{:S(2)}) async-start(f32[16,1,384]{2,1,0:T(1,128)} %reshape.197), calls=%async_computation.2 | async-start | bytes 49152 | tf_op jit(solution)/shard_map/all_to_all | solution.py:122
  60.3 0.0 collective-permute-done.2
  60.3 0.0 collective-permute-done.3
  60.3 1.4 %fusion.27 = (f32[8,1024,6]{1,0,2:T(8,128)S(1)}, f32[8,1024,6]{1,0,2:T(8,128)S(1)}, f32[8,1024,6]{1,0,2:T(8,128)S(1)}, f32[8,1024,6]{1,0,2:T(8,128)S(1)}) fusion(f32[6,8,1024]{2,1,0:T(8,128)} %bitcast.108, f32[6,1,1024]{2,1,0:T(1,128)} %collective-permute-done.2, f32[6,1,1024]{2,1,0:T(1,128)} %collective-permute-done.3), kind=kLoop, calls=%fused_computation.43 | loop fusion | flops 98304 | bytes 1032192
  61.8 1.4 %fusion.9 = (f32[8,1024,6]{1,0,2:T(8,128)}, f32[8,1024,6]{1,0,2:T(8,128)}, f32[8,1024,6]{1,0,2:T(8,128)}, f32[8,1024,6]{1,0,2:T(8,128)}) fusion(f32[8,1024,6]{1,0,2:T(8,128)S(1)} %get-tuple-element.67, bf16[4,6,6,8,1024]{4,3,2,1,0:T(8,128)(2,1)S(1)} %copy-done, f32[8,1024,6]{1,0,2:T(8,128)S(1)} %get-tuple-element.66, ...), kind=kLoop, calls=%fused_computation.19 | loop fusion | flops 3342336 | bytes 3932160 | tf_op jit(solution)/shard_map/abij,bij->aij/dot_general | solution.py:86
  63.2 3.7 %all-to-all-done.2 = f32[16,1,384]{2,1,0:T(1,128)} async-done(((f32[16,1,384]{2,1,0:T(1,128)}), f32[16,1,384]{2,1,0:T(1,128)}, u32[]{:S(2)}, u32[]{:S(2)}) %all-to-all-start.2) | async-done | bytes 24608 | tf_op jit(solution)/shard_map/all_to_all | solution.py:122
  67.0 1.4 %reduce.21 = f32[16,384]{1,0:T(8,128)S(1)} reduce(f32[16,1,384]{2,1,0:T(1,128)} %all-to-all-done.2, f32[]{:T(128)} %broadcast.187), dimensions={1}, to_apply=%all_to_all.11.reduce_sub_computation | reduce | bytes 49156 | tf_op jit(solution)/shard_map/all_to_all | solution.py:122
  68.4 0.2 reshape.198
  68.6 0.2 mul.159
  68.8 1.9 %fusion = f32[6,64,128]{2,1,0:T(8,128)S(1)} fusion(f32[6,1024]{1,0:T(8,128)S(1)} %mul.159, f32[1024,64]{0,1:T(8,128)} %fusion.23, s32[1024]{0:T(1024)S(1)} %copy-done.14), kind=kOutput, calls=%fused_computation | convolution fusion | flops 604504064 | bytes 487424 | tf_op jit(solution)/shard_map/while/body/eval_jaxpr/atb,to->abo/dot_general | solution.py:72
  70.8 0.0 copy-start.2
  70.9 0.0 copy-start.4
  70.9 0.1 fusion.33
  70.9 0.1 multiply_reduce_fusion
  71.1 0.7 copy-done.2
  71.8 0.1 copy-done.4
  71.9 0.8 multiply_reduce_fusion.3
  72.6 2.2 %maximum_dynamic-update-slice_fusion = f32[48]{0:T(128)S(1)} fusion(f32[48]{0:T(128)S(1)} %broadcast.166, u32[]{:T(128)} %bitcast.50, f32[1]{0:T(128)} %bitcast.49, f32[1]{0:T(128)} %bitcast.48, f32[1]{0:T(128)} %bitcast.47), kind=kLoop, calls=%fused_computation.86 | loop fusion | flops 6 | bytes 208
  74.8 30.1 %all-reduce.2 = f32[48]{0:T(128)S(1)} all-reduce(f32[48]{0:T(128)S(1)} %maximum_dynamic-update-slice_fusion), channel_id=2, replica_groups=mesh['design'=2,'blk'=16] {'blk'}, use_global_device_ids=true, to_apply=%add.2 | all-reduce | flops 48 | bytes 384
  105.0 0.1 reshape.167
  105.1 0.6 divide_sqrt_fusion
  (36 shorter events, 0.3 us)
Async XLA Ops:
  0.6 16.5 %copy-start.16 = (u32[32]{0:T(128)S(1)}, u32[32]{0:T(128)}, u32[]{:S(2)}) copy-start(u32[32]{0:T(128)} %constant.96) | copy-start | bytes 388
  0.6 26.5 %copy-start.3 = (f32[6,8,1024]{2,1,0:T(8,128)S(1)}, f32[6,8,1024]{2,1,0:T(8,128)}, u32[]{:S(2)}) copy-start(f32[6,8,1024]{2,1,0:T(8,128)} %param.9) | copy-start | bytes 589828
  0.7 15.6 %copy-start.11 = (f32[1,16,4,16]{3,2,1,0:T(4,128)S(1)}, f32[1,16,4,16]{3,2,1,0:T(4,128)}, u32[]{:S(2)}) copy-start(f32[1,16,4,16]{3,2,1,0:T(4,128)} %param.14) | copy-start | bytes 12292
  0.7 17.7 %all-to-all-start.1 = ((s32[16,4,16]{2,1,0:T(4,128)}), s32[16,4,16]{2,1,0:T(4,128)S(1)}, u32[]{:S(2)}, u32[]{:S(2)}) async-start(s32[16,4,16]{2,1,0:T(4,128)} %bitcast.114), calls=%async_computation.1 | async-start | bytes 65536 | tf_op jit(solution)/shard_map/all_to_all | solution.py:111
  9.3 17.9 %collective-permute-start = (f32[6,1,1024]{2,1,0:T(1,128)S(1)}, f32[6,1,1024]{2,1,0:T(1,128)S(1)}, u32[]{:S(2)}, u32[]{:S(2)}) collective-permute-start(f32[6,1,1024]{2,1,0:T(1,128)S(1)} %get-tuple-element.74), channel_id=1, source_target_pairs={{0,1},{1,2},{2,3},{3,4},{4,5},{5,6},{6,7},{7,8},{8,9},{9,10},{10,1... | collective-permute-start | bytes 73736 | tf_op jit(solution)/shard_map/ppermute | solution.py:16
  11.6 15.5 %collective-permute-start.1 = (f32[6,1,1024]{2,1,0:T(1,128)S(1)}, f32[6,1,1024]{2,1,0:T(1,128)S(1)}, u32[]{:S(2)}, u32[]{:S(2)}) collective-permute-start(f32[6,1,1024]{2,1,0:T(1,128)S(1)} %get-tuple-element.75), channel_id=1, source_target_pairs={{1,0},{2,1},{3,2},{4,3},{5,4},{6,5},{7,6},{8,7},{9,8},{10,9},{11,1... | collective-permute-start | bytes 73736 | tf_op jit(solution)/shard_map/ppermute | solution.py:19
  14.7 0.6 copy-start.15
  14.7 0.6 copy-start.12
  14.7 12.6 %copy-start = (bf16[4,6,6,8,1024]{4,3,2,1,0:T(8,128)(2,1)S(1)}, bf16[4,6,6,8,1024]{4,3,2,1,0:T(8,128)(2,1)}, u32[]{:S(2)}) copy-start(bf16[4,6,6,8,1024]{4,3,2,1,0:T(8,128)(2,1)} %param.11) | copy-start | bytes 7077892
  18.3 14.6 %all-to-all-start = ((f32[16,1,384]{2,1,0:T(1,128)}), f32[16,1,384]{2,1,0:T(1,128)S(1)}, u32[]{:S(2)}, u32[]{:S(2)}) async-start(f32[16,1,384]{2,1,0:T(1,128)} %reshape.195), calls=%async_computation | async-start | bytes 49152 | tf_op jit(solution)/shard_map/all_to_all | solution.py:122
  26.4 8.7 %copy-start.13 = (s32[1024]{0:T(1024)}, s32[1024]{0:T(1024)S(1)}, u32[]{:S(2)}) copy-start(s32[1024]{0:T(1024)S(1)} %get-tuple-element.76) | copy-start | bytes 12292
  35.1 6.4 %copy-start.1 = (f32[6,6,8,1024]{3,2,1,0:T(8,128)S(1)}, f32[6,6,8,1024]{3,2,1,0:T(8,128)}, u32[]{:S(2)}) copy-start(f32[6,6,8,1024]{3,2,1,0:T(8,128)} %param.10) | copy-start | bytes 3538948
  48.7 11.6 %collective-permute-start.2 = (f32[6,1,1024]{2,1,0:T(1,128)}, f32[6,1,1024]{2,1,0:T(1,128)}, u32[]{:S(2)}, u32[]{:S(2)}) collective-permute-start(f32[6,1,1024]{2,1,0:T(1,128)} %get-tuple-element.68), channel_id=1, source_target_pairs={{0,1},{1,2},{2,3},{3,4},{4,5},{5,6},{6,7},{7,8},{8,9},{9,10},{10,1... | collective-permute-start | bytes 73736 | tf_op jit(solution)/shard_map/ppermute | solution.py:16
  50.9 9.4 %collective-permute-start.3 = (f32[6,1,1024]{2,1,0:T(1,128)}, f32[6,1,1024]{2,1,0:T(1,128)}, u32[]{:S(2)}, u32[]{:S(2)}) collective-permute-start(f32[6,1,1024]{2,1,0:T(1,128)} %get-tuple-element.69), channel_id=1, source_target_pairs={{1,0},{2,1},{3,2},{4,3},{5,4},{6,5},{7,6},{8,7},{9,8},{10,9},{11,1... | collective-permute-start | bytes 73736 | tf_op jit(solution)/shard_map/ppermute | solution.py:19
  55.4 11.5 %all-to-all-start.2 = ((f32[16,1,384]{2,1,0:T(1,128)}), f32[16,1,384]{2,1,0:T(1,128)}, u32[]{:S(2)}, u32[]{:S(2)}) async-start(f32[16,1,384]{2,1,0:T(1,128)} %reshape.197), calls=%async_computation.2 | async-start | bytes 49152 | tf_op jit(solution)/shard_map/all_to_all | solution.py:122
  61.8 7.0 %copy-start.14 = (s32[1024]{0:T(1024)S(1)}, s32[1024]{0:T(1024)}, u32[]{:S(2)}) copy-start(s32[1024]{0:T(1024)} %copy-done.13) | copy-start | bytes 12292
  63.2 7.6 %copy-start.6 = (f32[6,8,1024]{2,1,0:T(8,128)S(1)}, f32[6,8,1024]{2,1,0:T(8,128)}, u32[]{:S(2)}) copy-start(f32[6,8,1024]{2,1,0:T(8,128)} %param.8) | copy-start | bytes 589828
  63.2 7.6 %copy-start.7 = (f32[8,1024,6]{1,0,2:T(8,128)S(1)}, f32[8,1024,6]{1,0,2:T(8,128)}, u32[]{:S(2)}) copy-start(f32[8,1024,6]{1,0,2:T(8,128)} %get-tuple-element.34) | copy-start | bytes 589828
  63.2 7.6 %copy-start.8 = (f32[8,1024,6]{1,0,2:T(8,128)S(1)}, f32[8,1024,6]{1,0,2:T(8,128)}, u32[]{:S(2)}) copy-start(f32[8,1024,6]{1,0,2:T(8,128)} %get-tuple-element.35) | copy-start | bytes 589828
  63.2 7.6 %copy-start.9 = (f32[8,1024,6]{1,0,2:T(8,128)S(1)}, f32[8,1024,6]{1,0,2:T(8,128)}, u32[]{:S(2)}) copy-start(f32[8,1024,6]{1,0,2:T(8,128)} %get-tuple-element.40) | copy-start | bytes 589828
  63.2 7.6 %copy-start.10 = (f32[8,1024,6]{1,0,2:T(8,128)S(1)}, f32[8,1024,6]{1,0,2:T(8,128)}, u32[]{:S(2)}) copy-start(f32[8,1024,6]{1,0,2:T(8,128)} %get-tuple-element.41) | copy-start | bytes 589828
  70.8 0.9 copy-start.2
  70.9 1.0 copy-start.4
  71.9 33.8 %copy-start.5 = (f32[8,1024,6]{1,0,2:T(8,128)}, f32[8,1024,6]{1,0,2:T(8,128)S(1)}, u32[]{:S(2)}) copy-start(f32[8,1024,6]{1,0,2:T(8,128)S(1)} %multiply_reduce_fusion) | copy-start | bytes 589828
